TPU v7x, 32 devices: a whole 2x2x4 slice. The times are simulated.
32 devices in a mesh: layer: 8 (over y, x, core), tensor: 4 (over z).
Axes of the slice: x: 2, y: 2, z: 4, core: 2. Of those that a mesh axis runs over, the one named last changes fastest.
Arguments:
- gradient: bfloat16 [8, 1024, 8192], P(None, 'tensor', 'layer'), may hold values from -8 to 8
- row_basis: bfloat16 [8, 1024, 256], P('layer', 'tensor'), may hold values from -0.1875 to 0.1875
- column_basis: bfloat16 [8, 8192, 256], P('layer', 'tensor'), may hold values from -0.0625 to 0.0625
- row_eigen: float32 [8, 256], P('layer'), may hold values from 0.01 to 10
- column_eigen: float32 [8, 256], P('layer'), may hold values from 0.01 to 10
- row_escape: float32 [8], P('layer'), may hold values from 0.02 to 0.2
- column_escape: float32 [8], P('layer'), may hold values from 0.02 to 0.2
Outputs:
- update: bfloat16 [8, 1024, 8192], P(None, 'tensor', 'layer')
All inputs are finite; a program needn't handle non-finite values.
Results may differ from a plain program's by a relative error of at most 0.0055.
Values may be sent and summed in bfloat16 or wider, within the bound.
A program may use at most 128 MiB of HBM per device.

v0:
```python
import jax
import jax.numpy as jnp
from jax import lax
from jax.sharding import PartitionSpec as P


def coefficients(row_eigen, column_eigen, row_escape, column_escape):
    row_base = row_escape ** (-0.25)
    column_base = column_escape ** (-0.25)
    row_coef = (row_eigen + row_escape[:, None]) ** (-0.25) - row_base[:, None]
    column_coef = (column_eigen + column_escape[:, None]) ** (-0.25) - column_base[:, None]
    return (row_base, column_base, row_coef, column_coef)


def group_norm(local_block):
    partial_sq = jnp.sum(jnp.square(local_block.astype(jnp.float32)), axis=(1, 2))
    return lax.psum(partial_sq, "tensor")


def finish(raw_update, grad_sq):
    update_sq = lax.psum(jnp.sum(jnp.square(raw_update), axis=(1, 2)), "tensor")
    factor = jnp.sqrt((grad_sq + 1.0) / (update_sq + 1.0))
    return (raw_update * factor[:, None, None]).astype(jnp.bfloat16)


def body(gradient, row_basis, column_basis, row_eigen, column_eigen, row_escape, column_escape):
    row_base, column_base, row_coef, column_coef = coefficients(
        row_eigen, column_eigen, row_escape, column_escape
    )
    both_base = (row_base * column_base)[:, None, None]
    group_block = lax.all_to_all(gradient, "layer", split_axis=0, concat_axis=2, tiled=True)
    grad_sq = group_norm(group_block)
    own_proj = lax.psum_scatter(
        jnp.einsum(
            "lrk,lrd->dlk", row_basis, group_block, preferred_element_type=jnp.float32
        ).astype(jnp.bfloat16),
        "tensor",
        scatter_dimension=0,
        tiled=True,
    ).astype(jnp.float32)
    scaled = (own_proj * row_coef[None]).astype(jnp.bfloat16)
    core_part = jnp.einsum("dlk,ldj->lkj", scaled, column_basis, preferred_element_type=jnp.float32)
    core_mat = lax.psum(core_part.astype(jnp.bfloat16), "tensor")
    whole_columns = lax.all_gather(column_basis, "tensor", axis=1, tiled=True)
    middle = jnp.einsum(
        "lrd,ldk->lrk", group_block, whole_columns, preferred_element_type=jnp.float32
    )
    row_term = jnp.einsum(
        "lrk,dlk->lrd",
        row_basis,
        lax.all_gather(scaled, "tensor", axis=0, tiled=True),
        preferred_element_type=jnp.float32,
    )
    mixed = row_base[:, None, None] * middle + jnp.einsum(
        "lrk,lkj->lrj", row_basis, core_mat, preferred_element_type=jnp.float32
    )
    left_factor = (mixed * column_coef[:, None, :]).astype(jnp.bfloat16)
    raw_update = both_base * group_block.astype(jnp.float32) + column_base[:, None, None] * row_term
    raw_update = raw_update + jnp.einsum(
        "lrk,ldk->lrd", left_factor, whole_columns, preferred_element_type=jnp.float32
    )
    rows_block = finish(raw_update, grad_sq)
    return lax.all_to_all(rows_block, "layer", split_axis=2, concat_axis=0, tiled=True)


def solution(mesh):
    in_specs = (
        P(None, "tensor", "layer"),
        P("layer", "tensor", None),
        P("layer", "tensor", None),
        P("layer", None),
        P("layer", None),
        P("layer"),
        P("layer"),
    )
    out_specs = P(None, "tensor", "layer")
    return jax.shard_map(body, mesh=mesh, in_specs=in_specs, out_specs=out_specs, check_vma=False)
```

profile of v0, /device:TPU:0, one launch (start us, length us, event | category | flops | bytes accessed | tf_op | source)
XLA Modules:
  0.0 558.4 jit_solution(9425964493506922182)
XLA Ops:
  6.5 54.5 %all_to_all.36 = bf16[8,256,1024]{2,1,0:T(8,128)(2,1)} all-to-all(bf16[8,256,1024]{2,1,0:T(8,128)(2,1)} %param.7), channel_id=1, replica_groups=mesh['layer'=8,'tensor'=4] {'layer'}, dimensions={0} | all-to-all | bytes 8388608 | tf_op jit(solution)/shard_map/all_to_all | solution.py:31
  61.0 6.4 %copy.15 = bf16[1,256,8,1024]{1,3,2,0:T(8,128)(2,1)} copy(bf16[1,256,8,1024]{3,1,2,0:T(8,128)(2,1)} %bitcast.80) | data formatting | bytes 8388608 | tf_op jit(solution)/shard_map/all_to_all | solution.py:31
  67.4 5.4 fusion.2
  72.9 0.7 all-gather.5.cloned.1.call-update
  74.4 75.4 %reduce-scatter.2.cloned.1.call-done = bf16[2048,1,256]{2,0,1:T(8,128)(2,1)} async-done(((bf16[8192,1,256]{2,0,1:T(8,128)(2,1)}), bf16[2048,1,256]{2,0,1:T(8,128)(2,1)}) %reduce-scatter.2.cloned.1.call-update) | async-done | bytes 1048592 | tf_op jit(solution)/shard_map/reduce_scatter | solution.py:33
  149.8 2.4 multiply_convert_fusion.1
  153.0 4.9 multiply_reduce_fusion.1
  158.0 74.7 %all-gather.5.cloned.1.call-done = bf16[1,8192,256]{2,1,0:T(8,128)(2,1)} async-done(((bf16[1,2048,256]{2,1,0:T(8,128)(2,1)}), bf16[1,8192,256]{2,1,0:T(8,128)(2,1)}) %all-gather.5.cloned.1.call-update) | async-done | bytes 4194320 | tf_op jit(solution)/shard_map/all_gather | solution.py:44
  232.7 4.8 fusion.10
  237.5 1.1 convolution_convert_fusion.1
  238.6 75.0 %all-gather.3.cloned.1.call-done = bf16[8192,1,256]{2,0,1:T(8,128)(2,1)} async-done(((bf16[2048,1,256]{2,0,1:T(8,128)(2,1)}), bf16[8192,1,256]{2,0,1:T(8,128)(2,1)}) %all-gather.3.cloned.1.call-update) | async-done | bytes 4194320 | tf_op jit(solution)/shard_map/all_gather | solution.py:51
  313.6 8.0 %fusion.1 = f32[256,8192]{0,1:T(8,128)} fusion(bf16[256,8192]{0,1:T(8,128)(2,1)} %bitcast.79, bf16[8192,1,256]{2,0,1:T(8,128)(2,1)} %all-gather.3.cloned.1.call-done, f32[]{:T(128)} %bitcast.4, f32[]{:T(128)} %bitcast, bf16[1,256,256]{2,1,0:T(8,128)(2,1)S(1)} %copy-done), kind=kOutput, calls=%fused_computation.3 | convolution fusion | flops 1082130432 | bytes 16908296 | tf_op jit(solution)/shard_map/lrk,dlk->lrd/dot_general | solution.py:48
  321.6 27.3 %all-reduce.3.cloned.1.call-done = bf16[256,256]{1,0:T(8,128)(2,1)} async-done(((bf16[256,256]{1,0:T(8,128)(2,1)}), bf16[256,256]{1,0:T(8,128)(2,1)}) %all-reduce.3.cloned.1.call-update) | async-done | bytes 131088 | tf_op jit(solution)/shard_map/psum | solution.py:43
  348.9 11.0 %multiply_reduce_fusion = (f32[]{:T(128)}, f32[256,8192]{0,1:T(8,128)}) fusion(f32[256,8192]{0,1:T(8,128)} %fusion.1, bf16[1,8192,256]{2,1,0:T(8,128)(2,1)} %all-gather.5.cloned.1.call-done, f32[256,256]{1,0:T(8,128)S(1)} %fusion.10, bf16[256,256]{1,0:T(8,128)(2,1)} %all-reduce.3.cloned.1.call-done, bf16[1,256,256]{2,1,0:T(8,128)(2,1)S(1)} %copy-done, ...), kind=kOutput, calls=%fused_computation.7 | convolution fusion | flops 1113784320 | bytes 21496836 | tf_op jit(solution)/shard_map/lrk,ldk->lrd/dot_general | solution.py:59
  359.9 11.3 %all-reduce = (f32[1]{0:T(128)}, f32[1]{0:T(128)}) all-reduce(f32[1]{0:T(128)} %bitcast.19, f32[1]{0:T(128)} %bitcast.20), channel_id=1, replica_groups=mesh['layer'=8,'tensor'=4] {'tensor'}, use_global_device_ids=true, to_apply=%region_3.0 | all-reduce | flops 2 | bytes 16 | tf_op jit(solution)/shard_map/psum | solution.py:17
  372.5 4.1 fusion.3
  376.5 49.5 %copy.24 = bf16[1,256,8192]{1,0,2:T(2,128)(2,1)} copy(bf16[1,256,8192]{1,2,0:T(8,128)(2,1)S(1)} %fusion.3) | data formatting | bytes 8388608 | tf_op jit(solution)/shard_map/convert_element_type | solution.py:23
  426.1 0.5 broadcast.23
  426.6 43.5 %reduce.4 = bf16[8192,256]{1,0:T(8,128)(2,1)} reduce(bf16[8192,1,256]{2,1,0:T(2,128)(2,1)} %bitcast.81, bf16[]{:T(256)} %broadcast.23), dimensions={1}, to_apply=%bitcast.74.reduce_sub_computation | reduce | bytes 8388610
  470.1 7.0 %reshape.90 = bf16[8,2,131072]{2,1,0:T(2,128)(2,1)} reshape(bf16[8192,256]{1,0:T(8,128)(2,1)} %reduce.4) | data formatting | bytes 8388608
  477.1 53.6 %all_to_all.37 = bf16[8,2,131072]{2,1,0:T(2,128)(2,1)} all-to-all(bf16[8,2,131072]{2,1,0:T(2,128)(2,1)} %reshape.90), channel_id=1, replica_groups=mesh['layer'=8,'tensor'=4] {'layer'}, dimensions={0} | all-to-all | bytes 8388608 | tf_op jit(solution)/shard_map/all_to_all | solution.py:63
  530.6 8.7 %reshape.91 = bf16[8192,1,256]{2,1,0:T(2,128)(2,1)} reshape(bf16[8,2,131072]{2,1,0:T(2,128)(2,1)} %all_to_all.37) | data formatting | bytes 8388608
  539.4 6.1 %copy.22 = bf16[1,256,8192]{1,2,0:T(8,128)(2,1)} copy(bf16[1,256,8192]{1,0,2:T(2,128)(2,1)} %bitcast.82) | data formatting | bytes 8388608
  545.4 6.5 %copy.19 = bf16[8,256,1024]{2,1,0:T(8,128)(2,1)} copy(bf16[8,256,1024]{1,2,0:T(8,128)(2,1)} %bitcast.83) | data formatting | bytes 8388608 | tf_op jit(solution)/shard_map/all_to_all | solution.py:63
  (21 shorter events, 0.2 us)
Async XLA Ops:
  6.5 60.9 %copy-start = (bf16[1,256,256]{2,1,0:T(8,128)(2,1)S(1)}, bf16[1,256,256]{2,1,0:T(8,128)(2,1)}, u32[]{:S(2)}) copy-start(bf16[1,256,256]{2,1,0:T(8,128)(2,1)} %param.8) | copy-start | bytes 393220
  6.5 143.3 %reduce-scatter.2.cloned.1.call-start = ((), (), s32[]{:S(2)}) async-start(), calls=%async_computation.3 | async-start | bytes 5242880 | tf_op jit(solution)/shard_map/reduce_scatter | solution.py:33
  72.8 1.5 copy-start.4
  72.8 80.2 %copy-start.5 = (f32[1,256]{1,0:T(1,128)S(1)}, f32[1,256]{1,0:T(1,128)}, u32[]{:S(2)}) copy-start(f32[1,256]{1,0:T(1,128)} %param.11) | copy-start | bytes 3076
  72.9 159.8 %all-gather.5.cloned.1.call-start = ((), (), s32[]{:S(2)}) async-start(), calls=%async_computation.5 | async-start | bytes 5242880 | tf_op jit(solution)/shard_map/all_gather | solution.py:44
  73.6 239.9 %all-gather.3.cloned.1.call-start = ((), (), s32[]{:S(2)}) async-start(), calls=%async_computation.4 | async-start | bytes 5242880 | tf_op jit(solution)/shard_map/all_gather | solution.py:51
  152.3 196.6 %all-reduce.3.cloned.1.call-start = ((), (), s32[]{:S(2)}) async-start(), calls=%async_computation.6 | async-start | bytes 262144 | tf_op jit(solution)/shard_map/psum | solution.py:43
  157.9 79.5 %copy-start.2 = (bf16[2048,1,256]{2,0,1:T(8,128)(2,1)S(1)}, bf16[2048,1,256]{2,0,1:T(8,128)(2,1)}, u32[]{:S(2)}) copy-start(bf16[2048,1,256]{2,0,1:T(8,128)(2,1)} %multiply_convert_fusion.1) | copy-start | bytes 3145732
  158.0 79.5 %copy-start.3 = (bf16[1,2048,256]{2,1,0:T(8,128)(2,1)S(1)}, bf16[1,2048,256]{2,1,0:T(8,128)(2,1)}, u32[]{:S(2)}) copy-start(bf16[1,2048,256]{2,1,0:T(8,128)(2,1)} %param.9) | copy-start | bytes 3145732
  545.4 6.5 %copy-start.1 = (bf16[1,256,256]{2,1,0:T(8,128)(2,1)S(1)}, bf16[1,256,256]{2,1,0:T(8,128)(2,1)}, u32[]{:S(2)}) copy-start(bf16[1,256,256]{2,1,0:T(8,128)(2,1)} %param.8) | copy-start | bytes 393220
Sparse Core Ops, SparseCore 0:
  73.0 76.7 reduce-scatter.1
  151.4 81.2 all-gather.4
  234.3 79.2 all-gather.2
  315.7 33.1 all-reduce.2
where the time goes:
time: 559 us; the launch traced here: 558 us
  waiting for transfers between devices  253 us (45%)
  blocking collectives  119 us (21%)
  local copies, waits for them, and re-layouts  84.7 us (15%)
  other arithmetic  54.9 us (10%)
  matrix products  30.3 us (5%)
  between operations  15.9 us (3%)
    reduce_scatter x1, waiting for transfers between devices, body(): lax.psum_scatter(jnp.einsum('lrk,lrd->dlk', row_basis, group_block, prefe...  75.4 us
    all_gather x1, waiting for transfers between devices, body(): lax.all_gather(scaled, 'tensor', axis=0, tiled=True)  75 us
    all_gather x1, waiting for transfers between devices, body(): whole_columns = lax.all_gather(column_basis, 'tensor', axis=1, tiled=True)  74.7 us
    all_to_all x1, blocking collectives, body(): lax.all_to_all(gradient, 'layer', split_axis=0, concat_axis=2, tiled=True)  54.5 us
    all_to_all x1, blocking collectives, body(): lax.all_to_all(rows_block, 'layer', split_axis=2, concat_axis=0, tiled=True)  53.6 us
    convert_element_type x1, local copies, waits for them, and re-layouts, finish(): return (raw_update * factor[:, None, None]).astype(jnp.bfloat16)  49.5 us
    unnamed x1, other arithmetic  43.5 us
    psum x1, waiting for transfers between devices, body(): core_mat = lax.psum(core_part.astype(jnp.bfloat16), 'tensor')  27.3 us
  transfers between devices with their start and end apart: 4, of which 4 were waited for; matrix products, arithmetic and copies ran while one was open for 4% of the time, Pallas kernels for 0%

commit v1 on v0

--- a/solution.py
+++ b/solution.py
@@ -41,7 +41,14 @@
     scaled = (own_proj * row_coef[None]).astype(jnp.bfloat16)
     core_part = jnp.einsum("dlk,ldj->lkj", scaled, column_basis, preferred_element_type=jnp.float32)
     core_mat = lax.psum(core_part.astype(jnp.bfloat16), "tensor")
-    whole_columns = lax.all_gather(column_basis, "tensor", axis=1, tiled=True)
+    ring = [column_basis]
+    for hop in range(3):
+        ring.append(lax.ppermute(ring[-1], "tensor", [(dev, (dev + 1) % 4) for dev in range(4)]))
+    whole_columns = jnp.roll(
+        jnp.concatenate(ring[::-1], axis=1),
+        (lax.axis_index("tensor") + 1) * ring[0].shape[1],
+        axis=1,
+    )
     middle = jnp.einsum(
         "lrd,ldk->lrk", group_block, whole_columns, preferred_element_type=jnp.float32
     )

time: 559 us -> 512 us (0.916)
  waiting for transfers between devices: 253 us -> 203 us
  local copies, waits for them, and re-layouts: 84.7 us -> 95.6 us
    ppermute x0 -> x3, waiting for transfers between devices: none -> 93.5 us  [body(): lax.ppermute(ring[-1], 'tensor', [(dev, (dev + 1) % 4) for dev in range(4)])]
    all_gather x1 -> x0, waiting for transfers between devices: 74.7 us -> none  [body(): whole_columns = lax.all_gather(column_basis, 'tensor', axis=1, tiled=True)]
    all_gather x1, waiting for transfers between devices: 75 us -> 33.4 us  [body(): lax.all_gather(scaled, 'tensor', axis=0, tiled=True)]
    psum x1, waiting for transfers between devices: 27.3 us -> 0.01 us  [body(): core_mat = lax.psum(core_part.astype(jnp.bfloat16), 'tensor')]
    unnamed x16 -> x25, local copies, waits for them, and re-layouts: 22.3 us -> 32.2 us
  transfers between devices with their start and end apart: 4 -> 6, of which waited for: 4 -> 5; matrix products, arithmetic and copies ran while one was open for 4% -> 4% of each run, Pallas kernels for 0% -> 0%
where the time goes in v1:
time: 512 us; the launch traced here: 511 us
  waiting for transfers between devices  203 us (40%)
  blocking collectives  117 us (23%)
  local copies, waits for them, and re-layouts  95.6 us (19%)
  other arithmetic  51.8 us (10%)
  matrix products  25.7 us (5%)
  between operations  15.9 us (3%)
    ppermute x3, waiting for transfers between devices, body(): lax.ppermute(ring[-1], 'tensor', [(dev, (dev + 1) % 4) for dev in range(4)])  93.5 us
    reduce_scatter x1, waiting for transfers between devices, body(): lax.psum_scatter(jnp.einsum('lrk,lrd->dlk', row_basis, group_block, prefe...  76.2 us
    all_to_all x1, blocking collectives, body(): lax.all_to_all(gradient, 'layer', split_axis=0, concat_axis=2, tiled=True)  54.5 us
    all_to_all x1, blocking collectives, body(): lax.all_to_all(rows_block, 'layer', split_axis=2, concat_axis=0, tiled=True)  53.5 us
    convert_element_type x1, local copies, waits for them, and re-layouts, finish(): return (raw_update * factor[:, None, None]).astype(jnp.bfloat16)  49.5 us
    unnamed x1, other arithmetic  43.4 us
    all_gather x1, waiting for transfers between devices, body(): lax.all_gather(scaled, 'tensor', axis=0, tiled=True)  33.4 us
    unnamed x25, local copies, waits for them, and re-layouts  32.2 us
  transfers between devices with their start and end apart: 6, of which 5 were waited for; matrix products, arithmetic and copies ran while one was open for 4% of the time, Pallas kernels for 0%

profile of v1, /device:TPU:0, one launch (start us, length us, event | category | flops | bytes accessed | tf_op | source)
XLA Modules:
  0.0 511.0 jit_solution(3349191325959335611)
XLA Ops:
  6.5 54.5 %all_to_all.36 = bf16[8,256,1024]{2,1,0:T(8,128)(2,1)} all-to-all(bf16[8,256,1024]{2,1,0:T(8,128)(2,1)} %param.7), channel_id=1, replica_groups=mesh['layer'=8,'tensor'=4] {'layer'}, dimensions={0} | all-to-all | bytes 8388608 | tf_op jit(solution)/shard_map/all_to_all | solution.py:31
  61.0 6.4 %copy.15 = bf16[1,256,8,1024]{1,3,2,0:T(8,128)(2,1)} copy(bf16[1,256,8,1024]{3,1,2,0:T(8,128)(2,1)} %bitcast.72) | data formatting | bytes 8388608 | tf_op jit(solution)/shard_map/all_to_all | solution.py:31
  67.4 5.5 %fusion.2 = bf16[8192,1,256]{2,0,1:T(8,128)(2,1)} fusion(bf16[256,8192]{0,1:T(8,128)(2,1)} %bitcast.69, bf16[1,256,256]{2,1,0:T(8,128)(2,1)S(1)} %copy-done), kind=kOutput, calls=%fused_computation.5 | convolution fusion | flops 1075838976 | bytes 8519680 | tf_op jit(solution)/shard_map/lrk,lrd->dlk/dot_general | solution.py:34
  73.7 76.2 %reduce-scatter.2.cloned.1.call-done = bf16[2048,1,256]{2,0,1:T(8,128)(2,1)} async-done(((bf16[8192,1,256]{2,0,1:T(8,128)(2,1)}), bf16[2048,1,256]{2,0,1:T(8,128)(2,1)}) %reduce-scatter.2.cloned.1.call-update) | async-done | bytes 1048592 | tf_op jit(solution)/shard_map/reduce_scatter | solution.py:33
  152.6 1.5 collective-permute-start
  154.2 27.0 %collective-permute-done = bf16[1,2048,256]{2,1,0:T(8,128)(2,1)S(1)} collective-permute-done((bf16[1,2048,256]{2,1,0:T(8,128)(2,1)S(1)}, bf16[1,2048,256]{2,1,0:T(8,128)(2,1)S(1)}, u32[]{:S(2)}, u32[]{:S(2)}) %collective-permute-start) | collective-permute-done | bytes 1048608 | tf_op jit(solution)/shard_map/ppermute | solution.py:46
  181.1 27.6 %collective-permute-done.1 = bf16[1,2048,256]{2,1,0:T(8,128)(2,1)S(1)} collective-permute-done((bf16[1,2048,256]{2,1,0:T(8,128)(2,1)S(1)}, bf16[1,2048,256]{2,1,0:T(8,128)(2,1)S(1)}, u32[]{:S(2)}, u32[]{:S(2)}) %collective-permute-start.1) | collective-permute-done | bytes 1048608 | tf_op jit(solution)/shard_map/ppermute | solution.py:46
  209.5 38.9 %collective-permute-done.2 = bf16[1,2048,256]{2,1,0:T(8,128)(2,1)} collective-permute-done((bf16[1,2048,256]{2,1,0:T(8,128)(2,1)S(1)}, bf16[1,2048,256]{2,1,0:T(8,128)(2,1)}, u32[]{:S(2)}, u32[]{:S(2)}) %collective-permute-start.2) | collective-permute-done | bytes 1048608 | tf_op jit(solution)/shard_map/ppermute | solution.py:46
  248.4 2.4 constant_dynamic-update-slice_fusion.7
  253.9 2.3 constant_dynamic-update-slice_fusion.3
  259.4 2.8 multiply_reduce_fusion.1
  263.3 4.8 fusion.19
  268.1 33.4 %all-gather.2.cloned.1.call-done = bf16[8192,1,256]{2,0,1:T(8,128)(2,1)} async-done(((bf16[2048,1,256]{2,0,1:T(8,128)(2,1)}), bf16[8192,1,256]{2,0,1:T(8,128)(2,1)}) %all-gather.2.cloned.1.call-update) | async-done | bytes 4194320 | tf_op jit(solution)/shard_map/all_gather | solution.py:58
  301.6 4.8 fusion.1
  306.4 8.3 %multiply_reduce_fusion = (f32[]{:T(128)}, f32[256,8192]{0,1:T(8,128)}) fusion(f32[256,8192]{0,1:T(8,128)S(1)} %fusion.1, bf16[256,256]{1,0:T(8,128)(2,1)S(1)} %fusion.19, bf16[1,16384,256]{2,1,0:T(8,128)(2,1)} %constant_dynamic-update-slice_fusion, s32[]{:T(128)S(6)} %select_n.14), kind=kOutput, calls=%fused_computation.7 | convolution fusion | flops 1080033280 | bytes 21102600 | tf_op jit(solution)/shard_map/lrk,ldk->lrd/dot_general | solution.py:66
  314.7 9.2 %all-reduce = (f32[1]{0:T(128)}, f32[1]{0:T(128)}) all-reduce(f32[1]{0:T(128)} %bitcast.18, f32[1]{0:T(128)} %bitcast.19), channel_id=1, replica_groups=mesh['layer'=8,'tensor'=4] {'tensor'}, use_global_device_ids=true, to_apply=%region_3.0 | all-reduce | flops 2 | bytes 16 | tf_op jit(solution)/shard_map/psum | solution.py:17
  325.2 4.1 fusion.3
  329.2 49.5 %copy.22 = bf16[1,256,8192]{1,0,2:T(2,128)(2,1)} copy(bf16[1,256,8192]{1,2,0:T(8,128)(2,1)S(1)} %fusion.3) | data formatting | bytes 8388608 | tf_op jit(solution)/shard_map/convert_element_type | solution.py:23
  379.2 43.4 %reduce.4 = bf16[8192,256]{1,0:T(8,128)(2,1)} reduce(bf16[8192,1,256]{2,1,0:T(2,128)(2,1)} %bitcast.73, bf16[]{:T(256)} %broadcast.27), dimensions={1}, to_apply=%bitcast.66.reduce_sub_computation | reduce | bytes 8388610
  422.7 7.0 %reshape.90 = bf16[8,2,131072]{2,1,0:T(2,128)(2,1)} reshape(bf16[8192,256]{1,0:T(8,128)(2,1)} %reduce.4) | data formatting | bytes 8388608
  429.6 53.5 %all_to_all.37 = bf16[8,2,131072]{2,1,0:T(2,128)(2,1)} all-to-all(bf16[8,2,131072]{2,1,0:T(2,128)(2,1)} %reshape.90), channel_id=1, replica_groups=mesh['layer'=8,'tensor'=4] {'layer'}, dimensions={0} | all-to-all | bytes 8388608 | tf_op jit(solution)/shard_map/all_to_all | solution.py:70
  483.2 8.8 %reshape.91 = bf16[8192,1,256]{2,1,0:T(2,128)(2,1)} reshape(bf16[8,2,131072]{2,1,0:T(2,128)(2,1)} %all_to_all.37) | data formatting | bytes 8388608
  491.9 6.1 %copy.20 = bf16[1,256,8192]{1,2,0:T(8,128)(2,1)} copy(bf16[1,256,8192]{1,0,2:T(2,128)(2,1)} %bitcast.74) | data formatting | bytes 8388608
  498.0 6.4 %copy.18 = bf16[8,256,1024]{2,1,0:T(8,128)(2,1)} copy(bf16[8,256,1024]{1,2,0:T(8,128)(2,1)} %bitcast.75) | data formatting | bytes 8388608 | tf_op jit(solution)/shard_map/all_to_all | solution.py:70
  (35 shorter events, 10.6 us)
Async XLA Ops:
  6.5 60.9 %copy-start = (bf16[1,256,256]{2,1,0:T(8,128)(2,1)S(1)}, bf16[1,256,256]{2,1,0:T(8,128)(2,1)}, u32[]{:S(2)}) copy-start(bf16[1,256,256]{2,1,0:T(8,128)(2,1)} %param.8) | copy-start | bytes 393220
  6.5 143.4 %reduce-scatter.2.cloned.1.call-start = ((), (), s32[]{:S(2)}) async-start(), calls=%async_computation.3 | async-start | bytes 5242880 | tf_op jit(solution)/shard_map/reduce_scatter | solution.py:33
  67.4 6.3 %copy-start.5 = (f32[1,256]{1,0:T(1,128)S(1)}, f32[1,256]{1,0:T(1,128)}, u32[]{:S(2)}) copy-start(f32[1,256]{1,0:T(1,128)} %param.10) | copy-start | bytes 3076
  67.4 83.9 %copy-start.3 = (bf16[1,2048,256]{2,1,0:T(8,128)(2,1)S(1)}, bf16[1,2048,256]{2,1,0:T(8,128)(2,1)}, u32[]{:S(2)}) copy-start(bf16[1,2048,256]{2,1,0:T(8,128)(2,1)} %param.9) | copy-start | bytes 3145732
  67.4 142.0 %copy-start.6 = (f32[1,256]{1,0:T(1,128)S(1)}, f32[1,256]{1,0:T(1,128)}, u32[]{:S(2)}) copy-start(f32[1,256]{1,0:T(1,128)} %param.11) | copy-start | bytes 3076
  73.0 189.2 %all-reduce.3.cloned.1.call-start = ((), (), s32[]{:S(2)}) async-start(), calls=%async_computation.5 | async-start | bytes 262144 | tf_op jit(solution)/shard_map/psum | solution.py:43
  151.4 2.8 copy-start.4
  152.5 149.1 %all-gather.2.cloned.1.call-start = ((), (), s32[]{:S(2)}) async-start(), calls=%async_computation.4 | async-start | bytes 5242880 | tf_op jit(solution)/shard_map/all_gather | solution.py:58
  152.6 28.6 %collective-permute-start = (bf16[1,2048,256]{2,1,0:T(8,128)(2,1)S(1)}, bf16[1,2048,256]{2,1,0:T(8,128)(2,1)S(1)}, u32[]{:S(2)}, u32[]{:S(2)}) collective-permute-start(bf16[1,2048,256]{2,1,0:T(8,128)(2,1)S(1)} %copy-done.3), channel_id=1, source_target_pairs={{0,1},{1,2},{2,3},{3,0},{4,5},{5,6},{6,7},{7,4},{8,9},{9,10},{10,1... | collective-permute-start | bytes 3145736 | tf_op jit(solution)/shard_map/ppermute | solution.py:46
  181.1 27.6 %collective-permute-start.1 = (bf16[1,2048,256]{2,1,0:T(8,128)(2,1)S(1)}, bf16[1,2048,256]{2,1,0:T(8,128)(2,1)S(1)}, u32[]{:S(2)}, u32[]{:S(2)}) collective-permute-start(bf16[1,2048,256]{2,1,0:T(8,128)(2,1)S(1)} %collective-permute-done), channel_id=1, source_target_pairs={{0,1},{1,2},{2,3},{3,0},{4,5},{5,6},{6,7},{7,4},{8,9},{9,10},{10,1... | collective-permute-start | bytes 3145736 | tf_op jit(solution)/shard_map/ppermute | solution.py:46
  208.8 39.6 %collective-permute-start.2 = (bf16[1,2048,256]{2,1,0:T(8,128)(2,1)S(1)}, bf16[1,2048,256]{2,1,0:T(8,128)(2,1)}, u32[]{:S(2)}, u32[]{:S(2)}) collective-permute-start(bf16[1,2048,256]{2,1,0:T(8,128)(2,1)S(1)} %collective-permute-done.1), channel_id=1, source_target_pairs={{0,1},{1,2},{2,3},{3,0},{4,5},{5,6},{6,7},{7,4},{8,9},{9,10},{10,1... | collective-permute-start | bytes 3145736 | tf_op jit(solution)/shard_map/ppermute | solution.py:46
  209.5 49.9 %copy-start.2 = (bf16[8,256,1024]{2,1,0:T(8,128)(2,1)S(1)}, bf16[8,256,1024]{2,1,0:T(8,128)(2,1)}, u32[]{:S(2)}) copy-start(bf16[8,256,1024]{2,1,0:T(8,128)(2,1)} %all_to_all.36) | copy-start | bytes 12582916
  491.9 12.5 %copy-start.1 = (bf16[1,256,256]{2,1,0:T(8,128)(2,1)S(1)}, bf16[1,256,256]{2,1,0:T(8,128)(2,1)}, u32[]{:S(2)}) copy-start(bf16[1,256,256]{2,1,0:T(8,128)(2,1)} %param.8) | copy-start | bytes 393220
Sparse Core Ops, SparseCore 0:
  73.1 76.7 reduce-scatter.1
  152.7 56.5 all-reduce.2
  210.8 90.7 all-gather.1
